TPU v7x, 32 devices: a whole 2x2x4 slice. The times are simulated.
32 devices in a mesh: chain: 8 (over y, x, core), col: 4 (over z).
Axes of the slice: x: 2, y: 2, z: 4, core: 2. Of those that a mesh axis runs over, the one named last changes fastest.
Arguments:
- rhs: bfloat16 [16, 64, 2560], P('chain', None, 'col'), may hold values from -6 to 6
- block_inverse: bfloat16 [16, 2560, 2560], P('chain', 'col'), as said below
- entry_factor: bfloat16 [16, 2560, 128], P('chain', 'col'), as said below
- exit_factor: bfloat16 [16, 2560, 128], P('chain', 'col'), as said below
- previous: bfloat16 [64, 2560], P(None, 'col'), may hold values from -6 to 6
Outputs:
- solution: float32 [16, 64, 2560], P('chain', None, 'col')
Inputs may be any that keep to these rules, and one draw needn't show every extreme that they name: Every block of block_inverse equals its own transpose. `entry_factor`: entries are independent, of mean zero. `exit_factor`: entries are independent, of mean zero.
All inputs are finite; a program needn't handle non-finite values.
Results may differ from a plain program's by a relative error of at most 0.0003.
Values may be sent and summed in bfloat16 or wider, within the bound.
A program may use at most 64 MiB of HBM per device.

v0:
```python
import jax
import jax.numpy as jnp
from jax import lax
from jax.sharding import PartitionSpec as P


def from_behind(block, axis, distance):
    devices = range(lax.axis_size(axis))
    route = [(i - distance, i) for i in devices if i - distance in devices]
    return lax.ppermute(block, axis, route)


def entering(part, axis, combine, identity, reverse):
    count = lax.axis_size(axis)
    place = lax.axis_index(axis)
    ahead = count - 1 - place if reverse else place
    gathered = jax.tree.map(lambda a: lax.all_gather(a, axis), part)
    state = jax.tree.map(lambda a, e: jnp.zeros_like(a) + jnp.asarray(e, a.dtype), part, identity)

    def one(step, state):
        source = count - 1 - step if reverse else step
        return combine(
            state, jax.tree.map(lambda a: lax.dynamic_index_in_dim(a, source, 0, False), gathered)
        )

    return lax.fori_loop(0, ahead, one, state)


def compose(earlier, later):
    exact = lax.Precision.HIGHEST
    first_map, first_shift = earlier
    second_map, second_shift = later
    return (
        jnp.dot(first_map, second_map, precision=exact),
        jnp.dot(first_shift, second_map, precision=exact) + second_shift,
    )


def shards(rhs, block_inverse, entry_factor, exit_factor, previous):
    exact = lax.Precision.HIGHEST
    intervals_here = rhs.shape[0]
    column_count = rhs.shape[1]
    state_width = entry_factor.shape[2]
    arriving = from_behind(exit_factor[:1], "chain", -1)
    following = jnp.concatenate([exit_factor[1:], arriving], axis=0)
    couple_part = -jnp.einsum(
        "irn,irm->inm", entry_factor, following, preferred_element_type=jnp.float32
    )
    source_part = jnp.einsum("icr,irm->icm", rhs, following, preferred_element_type=jnp.float32)
    opening_part = jnp.dot(previous, exit_factor[0], preferred_element_type=jnp.float32)
    couple, source, opening = lax.psum((couple_part, source_part, opening_part), "col")
    identity = jnp.eye(state_width, dtype=jnp.float32)
    empty_shift = jnp.zeros((column_count, state_width), jnp.float32)
    first_chain = lax.axis_index("chain") == 0
    matrix = identity
    offset = empty_shift
    for position in range(intervals_here):
        matrix = jnp.dot(matrix, couple[position], precision=exact)
        offset = jnp.dot(offset, couple[position], precision=exact) + source[position]
    folded = jnp.dot(opening, matrix, precision=exact) + offset
    offset = jnp.where(first_chain, folded, offset)
    matrix = jnp.where(first_chain, jnp.zeros_like(matrix), matrix)
    _, incoming = entering((matrix, offset), "chain", compose, (identity, empty_shift), False)
    carry_state = jnp.where(first_chain, opening, incoming)
    solved_list = []
    for position in range(intervals_here):
        solved_list.append(
            rhs[position].astype(jnp.float32)
            - jnp.dot(carry_state, entry_factor[position].astype(jnp.float32).T, precision=exact)
        )
        carry_state = jnp.dot(carry_state, couple[position], precision=exact) + source[position]
    forward = jnp.stack(solved_list).astype(jnp.bfloat16)
    applied = jnp.einsum(
        "icb,irb->icr",
        lax.all_gather(forward, "col", axis=2, tiled=True),
        block_inverse,
        preferred_element_type=jnp.float32,
    )
    carried_part = jnp.einsum(
        "icr,irn->icn",
        applied.astype(jnp.bfloat16),
        entry_factor,
        preferred_element_type=jnp.float32,
    )
    carried = lax.psum(carried_part, "col")
    last_chain = lax.axis_index("chain") == lax.axis_size("chain") - 1
    matrix = identity
    offset = empty_shift
    for position in reversed(range(intervals_here)):
        turned = couple[position].T
        matrix = jnp.dot(matrix, turned, precision=exact)
        offset = jnp.dot(offset, turned, precision=exact) + carried[position]
    matrix = jnp.where(last_chain, jnp.zeros_like(matrix), matrix)
    _, behind = entering((matrix, offset), "chain", compose, (identity, empty_shift), True)
    results = [None] * intervals_here
    for position in reversed(range(intervals_here)):
        results[position] = applied[position] - jnp.dot(
            behind, following[position].astype(jnp.float32).T, precision=exact
        )
        behind = jnp.dot(behind, couple[position].T, precision=exact) + carried[position]
    return jnp.stack(results)


def solution(mesh):
    placed = (
        P("chain", None, "col"),
        P("chain", "col", None),
        P("chain", "col", None),
        P("chain", "col", None),
        P(None, "col"),
    )
    return jax.shard_map(
        shards, mesh=mesh, in_specs=placed, out_specs=P("chain", None, "col"), check_vma=False
    )
```

profile of v0, /device:TPU:0, one launch (start us, length us, event | category | flops | bytes accessed | tf_op | source)
XLA Modules:
  0.0 161.5 jit_solution(1179635024437629665)
XLA Ops:
  6.5 1.1 fusion.37
  7.8 1.3 collective-permute-start
  9.3 1.8 %collective-permute-done = bf16[1,640,128]{1,2,0:T(8,128)(2,1)S(1)} collective-permute-done((bf16[1,640,128]{1,2,0:T(8,128)(2,1)S(1)}, bf16[1,640,128]{1,2,0:T(8,128)(2,1)S(1)}, u32[]{:S(2)}, u32[]{:S(2)}) %collective-permute-start) | collective-permute-done | bytes 163872 | tf_op jit(solution)/shard_map/ppermute | solution.py:10
  11.1 1.8 %convolution_bitcast_fusion.2 = f32[2,64,128]{2,1,0:T(8,128)} fusion(bf16[2,64,640]{2,1,0:T(8,128)(2,1)} %param.9, bf16[1,640,128]{1,2,0:T(8,128)(2,1)S(1)} %collective-permute-done, bf16[1,640,128]{1,2,0:T(8,128)(2,1)S(1)} %copy.11), kind=kOutput, calls=%fused_computation.23 | convolution fusion | flops 21135360 | bytes 557056 | tf_op jit(solution)/shard_map/icr,irm->icm/dot_general | solution.py:49
  12.9 1.9 %fusion.10 = f32[2,128,128]{1,2,0:T(8,128)} fusion(bf16[2,640,128]{2,1,0:T(8,128)(2,1)} %param.11, bf16[1,640,128]{1,2,0:T(8,128)(2,1)S(1)} %collective-permute-done, bf16[1,640,128]{1,2,0:T(8,128)(2,1)S(1)} %copy.11), kind=kOutput, calls=%fused_computation.17 | convolution fusion | flops 42139648 | bytes 786432 | tf_op jit(solution)/shard_map/irn,irm->inm/dot_general | solution.py:46
  14.8 1.1 fusion.17
  15.9 21.0 %psum.28 = f32[64,128]{1,0:T(8,128)S(1)} all-reduce(f32[64,128]{1,0:T(8,128)S(1)} %fusion.17), channel_id=1, replica_groups=mesh['chain'=8,'col'=4] {'col'}, use_global_device_ids=true, to_apply=%region_0.0 | all-reduce | flops 8192 | bytes 65536 | tf_op jit(solution)/shard_map/psum | solution.py:51
  36.9 18.5 %all-reduce.6.cloned.1.call-done = (f32[2,128,128]{1,2,0:T(8,128)}, f32[2,64,128]{2,1,0:T(8,128)}) async-done(((f32[2,128,128]{1,2,0:T(8,128)}, f32[2,64,128]{2,1,0:T(8,128)}), (f32[2,128,128]{1,2,0:T(8,128)}, f32[2,64,128]{2,1,0:T(8,128)})) %all-reduce.6.cloned.1.call-update) | async-done | bytes 196624 | tf_op jit(solution)/shard_map/psum | solution.py:51
  55.4 1.1 fusion.27
  56.5 1.1 convolution_add_fusion.5
  57.6 1.1 convolution_add_fusion.4
  58.7 1.1 broadcast_select_fusion
  60.0 9.2 %all-gather.1 = f32[512,128]{1,0:T(8,128)S(1)} all-gather(f32[64,128]{1,0:T(8,128)S(1)} %fusion.15), channel_id=3, replica_groups=mesh['chain'=8,'col'=4] {'chain'}, dimensions={0}, use_global_device_ids=true | all-gather | bytes 294912 | tf_op jit(solution)/shard_map/all_gather | solution.py:17
  69.2 9.8 %all-gather = f32[1024,128]{1,0:T(8,128)S(1)} all-gather(f32[128,128]{1,0:T(8,128)S(1)} %get-tuple-element.159), channel_id=2, replica_groups=mesh['chain'=8,'col'=4] {'chain'}, dimensions={0}, use_global_device_ids=true | all-gather | bytes 589824 | tf_op jit(solution)/shard_map/all_gather | solution.py:17
  79.3 1.1 convolution_add_fusion.3
  80.5 1.0 fusion.26
  81.9 17.2 %all_gather.31 = bf16[2,64,2560]{2,1,0:T(8,128)(2,1)S(1)} all-gather(bf16[2,64,640]{2,1,0:T(8,128)(2,1)S(1)} %pad_maximum_fusion.4), channel_id=1, replica_groups=mesh['chain'=8,'col'=4] {'col'}, dimensions={2}, use_global_device_ids=true | all-gather | bytes 819200 | tf_op jit(solution)/shard_map/all_gather | solution.py:75
  99.1 4.9 %fusion.38 = f32[2,64,640]{2,1,0:T(8,128)S(1)} fusion(bf16[2,64,2560]{2,1,0:T(8,128)(2,1)S(1)} %all_gather.31, bf16[2,640,2560]{2,1,0:T(8,128)(2,1)} %param.10), kind=kOutput, calls=%fused_computation.68 | convolution fusion | flops 419430400 | bytes 7536640 | tf_op jit(solution)/shard_map/icb,irb->icr/dot_general | solution.py:73
  105.1 9.9 %all-gather.2 = f32[1024,128]{1,0:T(8,128)S(1)} all-gather(f32[128,128]{1,0:T(8,128)S(1)} %convolution_select_fusion), channel_id=4, replica_groups=mesh['chain'=8,'col'=4] {'chain'}, dimensions={0}, use_global_device_ids=true | all-gather | bytes 589824 | tf_op jit(solution)/shard_map/all_gather | solution.py:17
  115.0 24.6 %all-reduce.4.cloned.1.call-done = f32[2,64,128]{2,1,0:T(8,128)} async-done(((f32[2,64,128]{2,1,0:T(8,128)}), f32[2,64,128]{2,1,0:T(8,128)}) %all-reduce.4.cloned.1.call-update) | async-done | bytes 65552 | tf_op jit(solution)/shard_map/psum | solution.py:85
  140.5 0.9 convolution_add_fusion.1
  141.5 9.3 %all-gather.3 = f32[512,128]{1,0:T(8,128)S(1)} all-gather(f32[64,128]{1,0:T(8,128)S(1)} %convolution_add_fusion.1), channel_id=5, replica_groups=mesh['chain'=8,'col'=4] {'chain'}, dimensions={0}, use_global_device_ids=true | all-gather | bytes 294912 | tf_op jit(solution)/shard_map/all_gather | solution.py:17
  150.8 1.6 %while.27 = (s32[]{:T(128)}, f32[64,128]{1,0:T(8,128)S(1)}, s32[]{:T(128)}, f32[8,128,128]{2,1,0:T(8,128)S(1)}, f32[8,64,128]{2,1,0:T(8,128)S(1)}, /*index=5*/s32[]{:T(128)}, s32[]{:T(128)}, s32[]{:T(128)}, s32[]{:T(128)}) while((s32[]{:T(128)}, f32[64,128]{1,0:T(8,128)S(1)}, s32[]{:T(128)}, f32[8,128,128]{2,1,0:T(8,128)S(1)}, ...), condition=%wide.region_7.8_spmd, body=%wide.region_6.7_spmd.sunk | while | flops 12591110 | bytes 230539 | solution.py:26
  152.4 0.9 convolution_add_fusion
  (43 shorter events, 5.9 us)
Async XLA Ops:
  6.5 8.3 %copy-start = (bf16[64,640]{1,0:T(8,128)(2,1)S(1)}, bf16[64,640]{1,0:T(8,128)(2,1)}, u32[]{:S(2)}) copy-start(bf16[64,640]{1,0:T(8,128)(2,1)} %param.13) | copy-start | bytes 245764
  6.5 72.5 %copy-start.4 = (bf16[2,64,640]{2,1,0:T(8,128)(2,1)S(1)}, bf16[2,64,640]{2,1,0:T(8,128)(2,1)}, u32[]{:S(2)}) copy-start(bf16[2,64,640]{2,1,0:T(8,128)(2,1)} %param.9) | copy-start | bytes 491524
  6.5 72.5 %copy-start.2 = (bf16[2,640,128]{2,1,0:T(8,128)(2,1)S(1)}, bf16[2,640,128]{2,1,0:T(8,128)(2,1)}, u32[]{:S(2)}) copy-start(bf16[2,640,128]{2,1,0:T(8,128)(2,1)} %param.11) | copy-start | bytes 983044
  6.5 48.9 %all-reduce.6.cloned.1.call-start = ((), (), s32[]{:S(2)}) async-start(), calls=%async_computation.1 | async-start | bytes 393216 | tf_op jit(solution)/shard_map/psum | solution.py:51
  7.8 3.3 %collective-permute-start = (bf16[1,640,128]{1,2,0:T(8,128)(2,1)S(1)}, bf16[1,640,128]{1,2,0:T(8,128)(2,1)S(1)}, u32[]{:S(2)}, u32[]{:S(2)}) collective-permute-start(bf16[1,640,128]{1,2,0:T(8,128)(2,1)S(1)} %copy.10), channel_id=1, source_target_pairs={{4,0},{8,4},{12,8},{16,12},{20,16},{24,20},{28,24},{5,1},{9,5},{13... | collective-permute-start | bytes 491528 | tf_op jit(solution)/shard_map/ppermute | solution.py:10
  14.8 124.8 %all-reduce.4.cloned.1.call-start = ((), (), s32[]{:S(2)}) async-start(), calls=%async_computation | async-start | bytes 131072 | tf_op jit(solution)/shard_map/psum | solution.py:85
  59.8 45.1 %copy-start.1 = (f32[2,128,128]{1,2,0:T(8,128)S(1)}, f32[2,128,128]{1,2,0:T(8,128)}, u32[]{:S(2)}) copy-start(f32[2,128,128]{1,2,0:T(8,128)} %get-tuple-element.155) | copy-start | bytes 393220
  79.3 74.0 %copy-start.3 = (bf16[2,640,128]{2,1,0:T(8,128)(2,1)S(1)}, bf16[2,640,128]{2,1,0:T(8,128)(2,1)}, u32[]{:S(2)}) copy-start(bf16[2,640,128]{2,1,0:T(8,128)(2,1)} %param.12) | copy-start | bytes 983044
Sparse Core Ops, SparseCore 0:
  14.9 40.4 all-reduce.5
  105.0 34.5 all-reduce.3
where the time goes:
time: 162 us; the launch traced here: 161 us
  blocking collectives  76.4 us (47%)
  waiting for transfers between devices  45 us (28%)
  matrix products  22.7 us (14%)
  between operations  13.6 us (8%)
    all_gather x4, blocking collectives, entering(): gathered = jax.tree.map(lambda a: lax.all_gather(a, axis), part)  38.2 us
    psum x1, waiting for transfers between devices, shards(): carried = lax.psum(carried_part, 'col')  24.6 us
    psum x1, blocking collectives, shards(): lax.psum((couple_part, source_part, opening_part), 'col')  21 us
    psum x1, waiting for transfers between devices, shards(): lax.psum((couple_part, source_part, opening_part), 'col')  18.5 us
    all_gather x1, blocking collectives, shards(): lax.all_gather(forward, 'col', axis=2, tiled=True)  17.2 us
    dot_general x1, matrix products, shards(): jnp.einsum('icb,irb->icr', lax.all_gather(forward, 'col', axis=2, tiled=T...  4.94 us
  transfers between devices with their start and end apart: 3, of which 3 were waited for; matrix products, arithmetic and copies ran while one was open for 1% of the time, Pallas kernels for 0%

commit v1 on v0

--- a/solution.py
+++ b/solution.py
@@ -70,11 +70,35 @@
         )
         carry_state = jnp.dot(carry_state, couple[position], precision=exact) + source[position]
     forward = jnp.stack(solved_list).astype(jnp.bfloat16)
-    applied = jnp.einsum(
-        "icb,irb->icr",
-        lax.all_gather(forward, "col", axis=2, tiled=True),
-        block_inverse,
-        preferred_element_type=jnp.float32,
+
+    def map_the_edge(incoming_x, on_dim, tile_in):
+        newest = lax.psum(1, "col")
+        now = lax.axis_index("col")
+        r2, inter, heard = (newest, now, incoming_x.shape[on_dim])
+        blocks_here = [(num, (num + 1) % r2) for num in range(r2)]
+        rows = [(num, (num - 1) % r2) for num in range(r2)]
+        base_arr = r2 // 2
+        step_out = tile_in(incoming_x, inter * heard)
+        y_new = out_arr = incoming_x
+        for p in range(1, base_arr + 1):
+            y_new = lax.ppermute(y_new, "col", blocks_here)
+            if p < r2 - base_arr:
+                out_arr = lax.ppermute(out_arr, "col", rows)
+                block_now = tile_in(out_arr, (inter + p) % r2 * heard)
+                step_out = step_out + block_now
+            carry_out = tile_in(y_new, (inter - p) % r2 * heard)
+            step_out = step_out + carry_out
+        return step_out
+
+    applied = map_the_edge(
+        forward,
+        2,
+        lambda own_block, start: jnp.einsum(
+            "icb,irb->icr",
+            own_block,
+            lax.dynamic_slice_in_dim(block_inverse, start, own_block.shape[2], axis=2),
+            preferred_element_type=jnp.float32,
+        ),
     )
     carried_part = jnp.einsum(
         "icr,irn->icn",

time: 162 us -> 156 us (0.963)
  blocking collectives: 76.4 us -> 59.2 us
  matrix products: 22.7 us -> 26.9 us
  starting transfers between devices: 1.34 us -> 5.21 us
  waiting for transfers between devices: 45 us -> 47.8 us
    all_gather x1 -> x0, blocking collectives: 17.2 us -> none  [shards(): lax.all_gather(forward, 'col', axis=2, tiled=True)]
    ppermute x0 -> x3, waiting for transfers between devices: none -> 4.02 us  [the longest x2 3.51 us: map_the_edge(): y_new = lax.ppermute(y_new, 'col', blocks_here)]
    ppermute x0 -> x3, starting transfers between devices: none -> 3.88 us  [the longest x1 2.27 us: map_the_edge(): out_arr = lax.ppermute(out_arr, 'col', rows)]
    dot_general x1 -> x4, matrix products: 4.94 us -> 8.32 us  [shards(): jnp.einsum('icb,irb->icr', own_block, lax.dynamic_slice_in_dim(block_inve...]
  transfers between devices with their start and end apart: 3 -> 6, of which waited for: 3 -> 6; matrix products, arithmetic and copies ran while one was open for 1% -> 6% of each run, Pallas kernels for 0% -> 0%
where the time goes in v1:
time: 156 us; the launch traced here: 155 us
  blocking collectives  59.2 us (38%)
  waiting for transfers between devices  47.8 us (31%)
  matrix products  26.9 us (17%)
  between operations  13.7 us (9%)
  starting transfers between devices  5.21 us (3%)
    all_gather x4, blocking collectives, entering(): gathered = jax.tree.map(lambda a: lax.all_gather(a, axis), part)  38.2 us
    psum x1, waiting for transfers between devices, shards(): carried = lax.psum(carried_part, 'col')  23.5 us
    psum x1, blocking collectives, shards(): lax.psum((couple_part, source_part, opening_part), 'col')  21 us
    psum x1, waiting for transfers between devices, shards(): lax.psum((couple_part, source_part, opening_part), 'col')  18.5 us
    dot_general x4, matrix products, shards(): jnp.einsum('icb,irb->icr', own_block, lax.dynamic_slice_in_dim(block_inve...  8.32 us
    ppermute x2, waiting for transfers between devices, map_the_edge(): y_new = lax.ppermute(y_new, 'col', blocks_here)  3.51 us
  transfers between devices with their start and end apart: 6, of which 6 were waited for; matrix products, arithmetic and copies ran while one was open for 6% of the time, Pallas kernels for 0%

profile of v1, /device:TPU:0, one launch (start us, length us, event | category | flops | bytes accessed | tf_op | source)
XLA Modules:
  0.0 155.3 jit_solution(13371388299988218290)
XLA Ops:
  6.5 1.1 fusion.66
  7.8 1.3 collective-permute-start
  9.3 1.7 %collective-permute-done = bf16[1,640,128]{1,2,0:T(8,128)(2,1)S(1)} collective-permute-done((bf16[1,640,128]{1,2,0:T(8,128)(2,1)S(1)}, bf16[1,640,128]{1,2,0:T(8,128)(2,1)S(1)}, u32[]{:S(2)}, u32[]{:S(2)}) %collective-permute-start) | collective-permute-done | bytes 163872 | tf_op jit(solution)/shard_map/ppermute | solution.py:10
  11.1 1.8 %convolution_bitcast_fusion.2 = f32[2,64,128]{2,1,0:T(8,128)} fusion(bf16[2,64,640]{2,1,0:T(8,128)(2,1)} %param.9, bf16[1,640,128]{1,2,0:T(8,128)(2,1)S(1)} %collective-permute-done, bf16[1,640,128]{1,2,0:T(8,128)(2,1)S(1)} %copy.11), kind=kOutput, calls=%fused_computation.30 | convolution fusion | flops 21135360 | bytes 557056 | tf_op jit(solution)/shard_map/icr,irm->icm/dot_general | solution.py:49
  12.9 1.9 %fusion.25 = f32[2,128,128]{1,2,0:T(8,128)} fusion(bf16[2,640,128]{2,1,0:T(8,128)(2,1)} %param.11, bf16[1,640,128]{1,2,0:T(8,128)(2,1)S(1)} %collective-permute-done, bf16[1,640,128]{1,2,0:T(8,128)(2,1)S(1)} %copy.11), kind=kOutput, calls=%fused_computation.24 | convolution fusion | flops 42139648 | bytes 786432 | tf_op jit(solution)/shard_map/irn,irm->inm/dot_general | solution.py:46
  15.9 21.0 %psum.28 = f32[64,128]{1,0:T(8,128)S(1)} all-reduce(f32[64,128]{1,0:T(8,128)S(1)} %fusion.39), channel_id=1, replica_groups=mesh['chain'=8,'col'=4] {'col'}, use_global_device_ids=true, to_apply=%region_0.0 | all-reduce | flops 8192 | bytes 65536 | tf_op jit(solution)/shard_map/psum | solution.py:51
  36.9 18.5 %all-reduce.6.cloned.1.call-done = (f32[2,128,128]{1,2,0:T(8,128)}, f32[2,64,128]{2,1,0:T(8,128)}) async-done(((f32[2,128,128]{1,2,0:T(8,128)}, f32[2,64,128]{2,1,0:T(8,128)}), (f32[2,128,128]{1,2,0:T(8,128)}, f32[2,64,128]{2,1,0:T(8,128)})) %all-reduce.6.cloned.1.call-update) | async-done | bytes 196624 | tf_op jit(solution)/shard_map/psum | solution.py:51
  56.5 1.1 convolution_add_fusion.5
  57.6 1.1 convolution_add_fusion.4
  58.7 1.1 broadcast_select_fusion
  60.0 9.2 %all-gather.1 = f32[512,128]{1,0:T(8,128)S(1)} all-gather(f32[64,128]{1,0:T(8,128)S(1)} %fusion.30), channel_id=3, replica_groups=mesh['chain'=8,'col'=4] {'chain'}, dimensions={0}, use_global_device_ids=true | all-gather | bytes 294912 | tf_op jit(solution)/shard_map/all_gather | solution.py:17
  69.2 9.8 %all-gather = f32[1024,128]{1,0:T(8,128)S(1)} all-gather(f32[128,128]{1,0:T(8,128)S(1)} %get-tuple-element.159), channel_id=2, replica_groups=mesh['chain'=8,'col'=4] {'chain'}, dimensions={0}, use_global_device_ids=true | all-gather | bytes 589824 | tf_op jit(solution)/shard_map/all_gather | solution.py:17
  79.3 1.1 convolution_add_fusion.3
  80.8 1.6 %collective-permute-start.2 = (bf16[2,64,640]{2,1,0:T(8,128)(2,1)S(1)}, bf16[2,64,640]{2,1,0:T(8,128)(2,1)S(1)}, u32[]{:S(2)}, u32[]{:S(2)}) collective-permute-start(bf16[2,64,640]{2,1,0:T(8,128)(2,1)S(1)} %pad_maximum_fusion.4), channel_id=1, source_target_pairs={{0,1},{1,2},{2,3},{3,0},{4,5},{5,6},{6,7},{7,4},{8,9},{9,10},{10,1... | collective-permute-start | bytes 491528 | tf_op jit(solution)/shard_map/ppermute | solution.py:84
  82.4 2.3 %collective-permute-start.1 = (bf16[2,64,640]{2,1,0:T(8,128)(2,1)S(1)}, bf16[2,64,640]{2,1,0:T(8,128)(2,1)S(1)}, u32[]{:S(2)}, u32[]{:S(2)}) collective-permute-start(bf16[2,64,640]{2,1,0:T(8,128)(2,1)S(1)} %pad_maximum_fusion.4), channel_id=1, source_target_pairs={{0,3},{1,0},{2,1},{3,2},{4,7},{5,4},{6,5},{7,6},{8,11},{9,8},{10,9... | collective-permute-start | bytes 491528 | tf_op jit(solution)/shard_map/ppermute | solution.py:86
  86.8 2.1 %fusion.14 = f32[2,64,640]{2,1,0:T(8,128)S(1)} fusion(bf16[2,640,2560]{2,1,0:T(8,128)(2,1)} %param.10, s32[]{:T(128)S(6)} %select_n.75, bf16[1,64,640]{2,1,0:T(8,128)(2,1)S(1)} %fusion.28, bf16[1,64,640]{2,1,0:T(8,128)(2,1)S(1)} %fusion.29), kind=kOutput, calls=%fused_computation.16 | convolution fusion | flops 104939520 | bytes 2129924 | tf_op jit(solution)/shard_map/icb,irb->icr/dot_general | solution.py:96
  89.8 2.1 %fusion.10 = f32[2,64,640]{2,1,0:T(8,128)S(1)} fusion(bf16[2,64,640]{2,1,0:T(8,128)(2,1)S(1)} %collective-permute-done.2, bf16[2,640,2560]{2,1,0:T(8,128)(2,1)} %param.10, s32[]{:T(128)S(6)} %select_n.79), kind=kOutput, calls=%fused_computation.12 | convolution fusion | flops 104857600 | bytes 2129924 | tf_op jit(solution)/shard_map/icb,irb->icr/dot_general | solution.py:96
  92.3 2.1 %fusion.19 = f32[2,64,640]{2,1,0:T(8,128)S(1)} fusion(f32[2,64,640]{2,1,0:T(8,128)S(1)} %fusion.10, f32[2,64,640]{2,1,0:T(8,128)S(1)} %fusion.14, bf16[2,64,640]{2,1,0:T(8,128)(2,1)S(1)} %collective-permute-done.1, bf16[2,640,2560]{2,1,0:T(8,128)(2,1)} %param.10, s32[]{:T(128)S(6)} %select_n.77), kind=kOutput, calls=%fused_computation.19 | convolution fusion | flops 105021440 | bytes 2785284 | tf_op jit(solution)/shard_map/icb,irb->icr/dot_general | solution.py:96
  94.4 2.6 %collective-permute-done.3 = bf16[2,64,640]{2,1,0:T(8,128)(2,1)S(1)} collective-permute-done((bf16[2,64,640]{2,1,0:T(8,128)(2,1)S(1)}, bf16[2,64,640]{2,1,0:T(8,128)(2,1)S(1)}, u32[]{:S(2)}, u32[]{:S(2)}) %collective-permute-start.3) | collective-permute-done | bytes 163872 | tf_op jit(solution)/shard_map/ppermute | solution.py:84
  97.0 2.1 %fusion.22 = f32[2,64,640]{2,1,0:T(8,128)S(1)} fusion(f32[2,64,640]{2,1,0:T(8,128)S(1)} %fusion.19, bf16[2,64,640]{2,1,0:T(8,128)(2,1)S(1)} %collective-permute-done.3, bf16[2,640,2560]{2,1,0:T(8,128)(2,1)} %param.10, s32[]{:T(128)S(6)} %select_n.81), kind=kOutput, calls=%fused_computation.20 | convolution fusion | flops 104939520 | bytes 2457604 | tf_op jit(solution)/shard_map/icb,irb->icr/dot_general | solution.py:96
  100.0 9.9 %all-gather.2 = f32[1024,128]{1,0:T(8,128)S(1)} all-gather(f32[128,128]{1,0:T(8,128)S(1)} %convolution_select_fusion), channel_id=4, replica_groups=mesh['chain'=8,'col'=4] {'chain'}, dimensions={0}, use_global_device_ids=true | all-gather | bytes 589824 | tf_op jit(solution)/shard_map/all_gather | solution.py:17
  109.9 23.5 %all-reduce.4.cloned.1.call-done = f32[2,64,128]{2,1,0:T(8,128)} async-done(((f32[2,64,128]{2,1,0:T(8,128)}), f32[2,64,128]{2,1,0:T(8,128)}) %all-reduce.4.cloned.1.call-update) | async-done | bytes 65552 | tf_op jit(solution)/shard_map/psum | solution.py:109
  135.3 9.3 %all-gather.3 = f32[512,128]{1,0:T(8,128)S(1)} all-gather(f32[64,128]{1,0:T(8,128)S(1)} %convolution_add_fusion.1), channel_id=5, replica_groups=mesh['chain'=8,'col'=4] {'chain'}, dimensions={0}, use_global_device_ids=true | all-gather | bytes 294912 | tf_op jit(solution)/shard_map/all_gather | solution.py:17
  144.5 1.6 %while.27 = (s32[]{:T(128)}, f32[64,128]{1,0:T(8,128)S(1)}, s32[]{:T(128)}, f32[8,128,128]{2,1,0:T(8,128)S(1)}, f32[8,64,128]{2,1,0:T(8,128)S(1)}, /*index=5*/s32[]{:T(128)}, s32[]{:T(128)}, s32[]{:T(128)}, s32[]{:T(128)}) while((s32[]{:T(128)}, f32[64,128]{1,0:T(8,128)S(1)}, s32[]{:T(128)}, f32[8,128,128]{2,1,0:T(8,128)S(1)}, ...), condition=%wide.region_7.8_spmd, body=%wide.region_6.7_spmd.sunk | while | flops 12591110 | bytes 230539 | solution.py:26
  (51 shorter events, 13.2 us)
Async XLA Ops:
  6.5 8.3 %copy-start = (bf16[64,640]{1,0:T(8,128)(2,1)S(1)}, bf16[64,640]{1,0:T(8,128)(2,1)}, u32[]{:S(2)}) copy-start(bf16[64,640]{1,0:T(8,128)(2,1)} %param.13) | copy-start | bytes 245764
  6.5 72.5 %copy-start.4 = (bf16[2,64,640]{2,1,0:T(8,128)(2,1)S(1)}, bf16[2,64,640]{2,1,0:T(8,128)(2,1)}, u32[]{:S(2)}) copy-start(bf16[2,64,640]{2,1,0:T(8,128)(2,1)} %param.9) | copy-start | bytes 491524
  6.5 72.5 %copy-start.2 = (bf16[2,640,128]{2,1,0:T(8,128)(2,1)S(1)}, bf16[2,640,128]{2,1,0:T(8,128)(2,1)}, u32[]{:S(2)}) copy-start(bf16[2,640,128]{2,1,0:T(8,128)(2,1)} %param.11) | copy-start | bytes 983044
  6.5 48.9 %all-reduce.6.cloned.1.call-start = ((), (), s32[]{:S(2)}) async-start(), calls=%async_computation.1 | async-start | bytes 393216 | tf_op jit(solution)/shard_map/psum | solution.py:51
  7.8 3.3 %collective-permute-start = (bf16[1,640,128]{1,2,0:T(8,128)(2,1)S(1)}, bf16[1,640,128]{1,2,0:T(8,128)(2,1)S(1)}, u32[]{:S(2)}, u32[]{:S(2)}) collective-permute-start(bf16[1,640,128]{1,2,0:T(8,128)(2,1)S(1)} %copy.10), channel_id=1, source_target_pairs={{4,0},{8,4},{12,8},{16,12},{20,16},{24,20},{28,24},{5,1},{9,5},{13... | collective-permute-start | bytes 491528 | tf_op jit(solution)/shard_map/ppermute | solution.py:10
  14.8 118.6 %all-reduce.4.cloned.1.call-start = ((), (), s32[]{:S(2)}) async-start(), calls=%async_computation | async-start | bytes 131072 | tf_op jit(solution)/shard_map/psum | solution.py:109
  79.0 54.4 %copy-start.1 = (f32[2,128,128]{1,2,0:T(8,128)S(1)}, f32[2,128,128]{1,2,0:T(8,128)}, u32[]{:S(2)}) copy-start(f32[2,128,128]{1,2,0:T(8,128)} %get-tuple-element.155) | copy-start | bytes 393220
  80.8 9.0 %collective-permute-start.2 = (bf16[2,64,640]{2,1,0:T(8,128)(2,1)S(1)}, bf16[2,64,640]{2,1,0:T(8,128)(2,1)S(1)}, u32[]{:S(2)}, u32[]{:S(2)}) collective-permute-start(bf16[2,64,640]{2,1,0:T(8,128)(2,1)S(1)} %pad_maximum_fusion.4), channel_id=1, source_target_pairs={{0,1},{1,2},{2,3},{3,0},{4,5},{5,6},{6,7},{7,4},{8,9},{9,10},{10,1... | collective-permute-start | bytes 491528 | tf_op jit(solution)/shard_map/ppermute | solution.py:84
  82.4 9.9 %collective-permute-start.1 = (bf16[2,64,640]{2,1,0:T(8,128)(2,1)S(1)}, bf16[2,64,640]{2,1,0:T(8,128)(2,1)S(1)}, u32[]{:S(2)}, u32[]{:S(2)}) collective-permute-start(bf16[2,64,640]{2,1,0:T(8,128)(2,1)S(1)} %pad_maximum_fusion.4), channel_id=1, source_target_pairs={{0,3},{1,0},{2,1},{3,2},{4,7},{5,4},{6,5},{7,6},{8,11},{9,8},{10,9... | collective-permute-start | bytes 491528 | tf_op jit(solution)/shard_map/ppermute | solution.py:86
  86.7 60.4 %copy-start.3 = (bf16[2,640,128]{2,1,0:T(8,128)(2,1)S(1)}, bf16[2,640,128]{2,1,0:T(8,128)(2,1)}, u32[]{:S(2)}) copy-start(bf16[2,640,128]{2,1,0:T(8,128)(2,1)} %param.12) | copy-start | bytes 983044
  89.8 7.3 %collective-permute-start.3 = (bf16[2,64,640]{2,1,0:T(8,128)(2,1)S(1)}, bf16[2,64,640]{2,1,0:T(8,128)(2,1)S(1)}, u32[]{:S(2)}, u32[]{:S(2)}) collective-permute-start(bf16[2,64,640]{2,1,0:T(8,128)(2,1)S(1)} %collective-permute-done.2), channel_id=1, source_target_pairs={{0,1},{1,2},{2,3},{3,0},{4,5},{5,6},{6,7},{7,4},{8,9},{9,10},{10,1... | collective-permute-start | bytes 491528 | tf_op jit(solution)/shard_map/ppermute | solution.py:84
Sparse Core Ops, SparseCore 0:
  14.9 40.4 all-reduce.5
  100.1 33.2 all-reduce.3
